TPU v7x, 32 devices: a whole 2x2x4 slice. The times are simulated.
32 devices in a mesh: replica: 8 (over z, y), fsdp: 4 (over x, core).
Axes of the slice: x: 2, y: 2, z: 4, core: 2. Of those that a mesh axis runs over, the one named last changes fastest.
Arguments:
- activations: bfloat16 [8, 4096, 4096], P('replica', 'fsdp')
- cotangents: bfloat16 [8, 4096, 512], P('replica', 'fsdp'), may hold values from -0.059814453 to 0.059814453
- momentum: float32 [8, 4096, 512], P('replica', 'fsdp'), may hold values from -6 to 6
- keep_index: int32 [8, 512, 32], P(None, 'fsdp'), may hold values from 0 to 4095, as said below
Outputs:
- new_momentum: float32 [8, 4096, 512], P('replica', 'fsdp')
- update: bfloat16 [4096, 512], P('fsdp')
Inputs may be any that keep to these rules, and one draw needn't show every extreme that they name: keep_index[r, t, j] lies in [j * 64 * 2, (j + 1) * 64 * 2), so a tile's indices are distinct and ascending.
All inputs are finite; a program needn't handle non-finite values.
Results may differ from a plain program's by a relative error of at most 0.013.
Values may be sent and summed in bfloat16 or wider, within the bound.
No kernel may reach another device: no remote copies, remote signals or barrier semaphores. Data moves between devices by JAX's collectives and lax.ppermute only.
A program may use at most 128 MiB of HBM per device.

v0:
```python
import jax
import jax.numpy as jnp
from jax import lax
from jax.sharding import PartitionSpec as P

D_WIN = 4096
KV_WIN = 512
TILE = 64
KEEP = 32


BETA = 0.999
EPS = 1e-06
highest = lax.Precision.HIGHEST


def cosine_table():
    sample = jnp.arange(TILE).astype(jnp.float32)
    freq_index = sample[:, None]
    table = jnp.cos(jnp.pi * (2.0 * sample[None, :] + 1.0) * freq_index / (2.0 * TILE))
    weight_row = jnp.where(freq_index == 0, jnp.sqrt(1.0 / TILE), jnp.sqrt(2.0 / TILE))
    return table * weight_row


def forward_tiled(matrix, cosine):
    row_count, col_count = matrix.shape
    blocks = matrix.reshape(row_count // TILE, TILE, col_count // TILE, TILE)
    left = jnp.einsum("ka,iajb->ijkb", cosine, blocks, precision=highest)
    spectra = jnp.einsum("ijkb,lb->ijkl", left, cosine, precision=highest)
    band = TILE * TILE // KEEP
    return spectra.reshape(row_count // TILE * (col_count // TILE), KEEP, band)


def inverse_tiled(tiled, cosine, row_count, col_count):
    blocks = tiled.reshape(row_count // TILE, col_count // TILE, TILE, TILE)
    left = jnp.einsum("ka,ijkl->ijal", cosine, blocks, precision=highest)
    return jnp.einsum("ijal,lb->iajb", left, cosine, precision=highest).reshape(
        row_count, col_count
    )


def band_mask(indices):
    band = TILE * TILE // KEEP
    offsets = indices - jnp.arange(KEEP)[None, :] * band
    slots = jnp.arange(band)
    return (offsets[:, :, None] == slots[None, None, :]).astype(jnp.float32)


def shards(activations, cotangents, momentum, keep_index):
    cosine = cosine_table()
    tokens_here = activations[0]
    grads_here = cotangents[0]
    local_rows = momentum.shape[1]
    gradient = lax.psum_scatter(
        lax.dot_general(
            tokens_here, grads_here, (((0,), (0,)), ((), ())), preferred_element_type=jnp.float32
        ).astype(jnp.bfloat16),
        "fsdp",
        scatter_dimension=0,
        tiled=True,
    ).astype(jnp.float32)
    moment = BETA * momentum[0] + gradient
    spectrum = forward_tiled(moment, cosine)
    own_index = lax.dynamic_index_in_dim(keep_index, lax.axis_index("replica"), 0, keepdims=False)
    own_mask = band_mask(own_index)
    sent_tiles = spectrum * own_mask
    kept_coeffs = jnp.sum(sent_tiles, axis=2)
    new_moment = moment - inverse_tiled(sent_tiles, cosine, local_rows, KV_WIN)
    shaped = kept_coeffs.reshape(1, kept_coeffs.shape[0], kept_coeffs.shape[1])
    pieces = lax.all_gather(shaped, "replica", axis=0, tiled=True)

    def add_one(step, total):
        values = lax.dynamic_index_in_dim(pieces, step, 0, keepdims=False)
        chosen = lax.dynamic_index_in_dim(keep_index, step, 0, keepdims=False)
        return total + band_mask(chosen) * values[:, :, None]

    summed = lax.fori_loop(0, pieces.shape[0], add_one, jnp.zeros_like(spectrum))
    replica_count = lax.axis_size("replica")
    merged = inverse_tiled(summed, cosine, local_rows, KV_WIN) / replica_count
    square_total = lax.psum(jnp.sum(merged * merged), "fsdp")
    scale_factor = lax.rsqrt(square_total / (D_WIN * KV_WIN) + EPS)
    update = (merged * scale_factor).astype(jnp.bfloat16)
    return (new_moment[None], update)


def solution(mesh):
    in_specs = (
        P("replica", "fsdp", None),
        P("replica", "fsdp", None),
        P("replica", "fsdp", None),
        P(None, "fsdp", None),
    )
    out_specs = (P("replica", "fsdp", None), P("fsdp", None))
    return jax.shard_map(shards, mesh=mesh, in_specs=in_specs, out_specs=out_specs, check_vma=False)
```

profile of v0, /device:TPU:0, one launch (start us, length us, event | category | flops | bytes accessed | tf_op | source)
XLA Modules:
  0.0 206.3 jit_solution(808510210893319870)
XLA Ops:
  7.2 0.0 copy-start
  7.2 0.0 reduce-scatter.2.cloned.1.call-start
  7.2 1.2 copy-done
  8.4 9.8 %fusion.2 = bf16[4096,512]{1,0:T(8,128)(2,1)} fusion(bf16[1,1024,4096]{2,1,0:T(8,128)(2,1)} %param.6, bf16[1,1024,512]{2,1,0:T(8,128)(2,1)S(1)} %copy-done), kind=kOutput, calls=%fused_computation.8 | convolution fusion | flops 4297064448 | bytes 13631488 | tf_op jit(solution)/shard_map/dot_general | solution.py:55
  18.2 0.0 reduce-scatter.2.cloned.1.call-update
  18.2 0.1 copy.16
  18.3 0.8 bitcast_subtract_fusion.1
  19.1 0.3 eq.86
  19.4 0.2 copy.15
  19.7 45.9 %reduce-scatter.2.cloned.1.call-done = bf16[1024,512]{1,0:T(8,128)(2,1)} async-done(((bf16[4096,512]{1,0:T(8,128)(2,1)}), bf16[1024,512]{1,0:T(8,128)(2,1)}) %reduce-scatter.2.cloned.1.call-update) | async-done | bytes 1048592 | tf_op jit(solution)/shard_map/reduce_scatter | solution.py:54
  65.6 3.6 %bitcast_add_fusion = f32[1024,512]{1,0:T(8,128)} fusion(bf16[1024,512]{1,0:T(8,128)(2,1)} %reduce-scatter.2.cloned.1.call-done, f32[1,1024,512]{2,1,0:T(8,128)} %param.8), kind=kLoop, calls=%fused_computation.24 | loop fusion | flops 1572864 | bytes 5242880 | tf_op jit(solution)/shard_map/add | solution.py:62
  69.2 4.4 %reshape.103 = f32[16,64,8,64]{3,2,1,0:T(8,128)} reshape(f32[1024,512]{1,0:T(8,128)} %bitcast_add_fusion) | data formatting | bytes 4194304 | tf_op jit(solution)/shard_map/reshape | solution.py:27
  73.6 9.4 %fusion.11 = f32[16,8,64,64]{3,2,1,0:T(8,128)S(1)} fusion(f32[16,64,8,64]{3,2,1,0:T(8,128)} %reshape.103, f32[64]{0:T(128)S(1)} %get-tuple-element.121, f32[64]{0:T(128)S(1)} %iota_convert_fusion, f32[64]{0:T(128)S(1)} %get-tuple-element.122), kind=kOutput, calls=%fused_computation.15 | convolution fusion | flops 402665472 | bytes 4195072 | tf_op jit(solution)/shard_map/ka,iajb->ijkb/dot_general | solution.py:28
  83.0 4.9 %fusion.13 = (f32[16,8,64]{2,1,0:T(8,128)S(1)}, f32[16,8,64,64]{2,3,1,0:T(8,128)S(1)}) fusion(s32[64,64]{0,1:T(8,128)S(1)} %copy.16, s32[16,8,64]{2,1,0:T(8,128)S(1)} %copy.15, f32[64]{0:T(128)S(1)} %get-tuple-element.121, f32[64]{0:T(128)S(1)} %iota_convert_fusion, f32[64]{0:T(128)S(1)} %get-tuple-element.122, f32[16,8,64,64]{3,2,1,0:T(8,128)S(1)} %fusion.11), kind=kOutput, calls=%fused_computation.20 | convolution fusion | flops 404230144 | bytes 4276992 | tf_op jit(solution)/shard_map/ijkb,lb->ijkl/dot_general | solution.py:29
  87.9 3.8 %fusion.14 = f32[16,8,64,64]{3,2,1,0:T(8,128)S(1)} fusion(f32[16,8,64,64]{2,3,1,0:T(8,128)S(1)} %get-tuple-element.118, s32[64,64]{0,1:T(8,128)S(1)} %copy.16, s32[16,8,64]{2,1,0:T(8,128)S(1)} %copy.15, f32[64]{0:T(128)S(1)} %get-tuple-element.121, f32[64]{0:T(128)S(1)} %iota_convert_fusion, f32[64]{0:T(128)S(1)} %get-tuple-element.122), kind=kOutput, calls=%fused_computation.21 | convolution fusion | flops 403714048 | bytes 4244224 | tf_op jit(solution)/shard_map/ka,ijkl->ijal/dot_general | solution.py:36
  91.7 5.6 %fusion.15 = f32[16,64,8,64]{1,3,2,0:T(8,128)} fusion(f32[16,8,64,64]{3,2,1,0:T(8,128)S(1)} %fusion.14, f32[64]{0:T(128)S(1)} %get-tuple-element.121, f32[64]{0:T(128)S(1)} %iota_convert_fusion, f32[64]{0:T(128)S(1)} %get-tuple-element.122), kind=kOutput, calls=%fused_computation.22 | convolution fusion | flops 402665472 | bytes 4195072 | tf_op jit(solution)/shard_map/ijal,lb->iajb/dot_general | solution.py:37
  97.3 5.3 %copy.23 = f32[16,64,8,64]{3,2,1,0:T(8,128)} copy(f32[16,64,8,64]{1,3,2,0:T(8,128)} %fusion.15) | data formatting | bytes 4194304 | tf_op jit(solution)/shard_map/ijal,lb->iajb/transpose | solution.py:37
  102.7 4.8 %reshape.104 = f32[1024,512]{1,0:T(8,128)} reshape(f32[16,64,8,64]{3,2,1,0:T(8,128)} %copy.23) | data formatting | bytes 4194304 | tf_op jit(solution)/shard_map/reshape | solution.py:37
  107.5 4.0 %subtract_bitcast_fusion = f32[1,1024,512]{2,1,0:T(8,128)} fusion(f32[1024,512]{1,0:T(8,128)} %bitcast_add_fusion, f32[1024,512]{1,0:T(8,128)} %reshape.104), kind=kLoop, calls=%fused_computation.25 | loop fusion | flops 524288 | bytes 6291456 | tf_op jit(solution)/shard_map/broadcast_in_dim | solution.py:83
  111.5 0.3 copy.24
  111.8 0.3 reduce_sum.26
  112.1 30.6 %all-gather = f32[1024,32]{0,1:T(8,128)S(1)} all-gather(f32[128,32]{0,1:T(8,128)S(1)} %reduce_sum.27), channel_id=2, replica_groups=mesh['replica'=8,'fsdp'=4] {'replica'}, dimensions={0}, use_global_device_ids=true | all-gather | bytes 147456 | tf_op jit(solution)/shard_map/all_gather | solution.py:70
  142.7 0.2 copy.43
  142.9 19.4 %while.14 = (s32[]{:T(128)}, f32[128,32,128]{2,1,0:T(8,128)S(1)}, s32[8,128,32]{1,2,0:T(8,128)}, f32[8,128,32]{2,1,0:T(8,128)S(1)}, s32[]{:T(128)}, /*index=5*/s32[]{:T(128)}) while((s32[]{:T(128)}, f32[128,32,128]{2,1,0:T(8,128)S(1)}, s32[8,128,32]{1,2,0:T(8,128)}, f32[8,128,32]{2,1,0:T(8,128)S(1)}, s32[]{:T(128)}, ...), condition=%wide.region_4.5_spmd.clone, body=%wide.region_3.4_spmd.clone.sunk | while | flops 2101283 | bytes 4358495 | solution.py:77
  142.9 0.7 constant_dynamic-slice_fusion.2
  143.6 0.1 copy.49
  143.8 1.5 select_add_fusion.2
  145.3 0.7 constant_dynamic-slice_fusion.2
  146.1 0.1 copy.49
  146.2 1.5 select_add_fusion.2
  147.8 0.7 constant_dynamic-slice_fusion.2
  148.5 0.1 copy.49
  148.6 1.5 select_add_fusion.2
  150.2 0.7 constant_dynamic-slice_fusion.2
  150.9 0.1 copy.49
  151.0 1.5 select_add_fusion.2
  152.6 0.7 constant_dynamic-slice_fusion.2
  153.3 0.1 copy.49
  153.5 1.5 select_add_fusion.2
  155.0 0.7 constant_dynamic-slice_fusion.2
  155.7 0.1 copy.49
  155.9 1.5 select_add_fusion.2
  157.4 0.7 constant_dynamic-slice_fusion.2
  158.2 0.1 copy.49
  158.3 1.5 select_add_fusion.2
  159.9 0.7 constant_dynamic-slice_fusion.2
  160.6 0.1 copy.49
  160.7 1.5 select_add_fusion.2
  162.3 2.3 %reshape.106 = f32[16,8,64,64]{3,2,1,0:T(8,128)} reshape(f32[128,32,128]{2,1,0:T(8,128)S(1)} %get-tuple-element.81) | data formatting | bytes 4194304 | tf_op jit(solution)/shard_map/reshape | solution.py:35
  164.6 8.7 %fusion.23 = f32[16,8,64,64]{3,2,1,0:T(8,128)S(1)} fusion(f32[16,8,64,64]{3,2,1,0:T(8,128)} %reshape.106, f32[64]{0:T(128)S(1)} %get-tuple-element.121, f32[64]{0:T(128)S(1)} %iota_convert_fusion, f32[64]{0:T(128)S(1)} %get-tuple-element.122), kind=kOutput, calls=%fused_computation.30 | convolution fusion | flops 402665472 | bytes 4195072 | tf_op jit(solution)/shard_map/ka,ijkl->ijal/dot_general | solution.py:36
  173.3 6.6 %multiply_reduce_fusion = (f32[]{:T(128)}, f32[64,16,8,64]{3,0,2,1:T(8,128)}) fusion(f32[16,8,64,64]{3,2,1,0:T(8,128)S(1)} %fusion.23, f32[64]{0:T(128)S(1)} %get-tuple-element.121, f32[64]{0:T(128)S(1)} %iota_convert_fusion, f32[64]{0:T(128)S(1)} %get-tuple-element.122), kind=kOutput, calls=%fused_computation.18 | convolution fusion | flops 404238336 | bytes 4195076 | tf_op jit(solution)/shard_map/ijal,lb->iajb/dot_general | solution.py:37
  179.9 6.5 %psum.7 = f32[]{:T(128)} all-reduce(f32[]{:T(128)} %get-tuple-element.119), channel_id=1, replica_groups=mesh['replica'=8,'fsdp'=4] {'fsdp'}, use_global_device_ids=true, to_apply=%region_6.7 | all-reduce | flops 1 | bytes 8 | tf_op jit(solution)/shard_map/psum | solution.py:80
  187.1 0.0 copy-start.1
  187.1 4.2 %fusion.18 = bf16[16,64,8,64]{1,3,2,0:T(8,128)(2,1)} fusion(f32[64,16,8,64]{3,0,2,1:T(8,128)} %get-tuple-element.120, f32[]{:T(128)S(6)} %mul.197), kind=kLoop, calls=%fused_computation.23 | loop fusion | flops 1048576 | bytes 3145732 | tf_op jit(solution)/shard_map/convert_element_type | solution.py:82
  191.3 4.1 %copy.30 = bf16[16,64,8,64]{3,2,1,0:T(8,128)(2,1)} copy(bf16[16,64,8,64]{1,3,2,0:T(8,128)(2,1)} %fusion.18) | data formatting | bytes 2097152 | tf_op jit(solution)/shard_map/convert_element_type | solution.py:82
  195.4 4.0 %convert_element_type.48 = bf16[1024,512]{1,0:T(8,128)(2,1)} reshape(bf16[16,64,8,64]{3,2,1,0:T(8,128)(2,1)} %copy.30) | data formatting | bytes 2097152 | tf_op jit(solution)/shard_map/convert_element_type | solution.py:82
  199.5 0.0 copy-done.1
  (32 shorter events, 0.3 us)
Async XLA Ops:
  7.2 1.2 copy-start
  7.2 58.4 %reduce-scatter.2.cloned.1.call-start = ((), (), s32[]{:S(2)}) async-start(), calls=%async_computation.1 | async-start | bytes 5242880 | tf_op jit(solution)/shard_map/reduce_scatter | solution.py:54
  187.1 12.4 %copy-start.1 = (bf16[1,1024,512]{2,1,0:T(8,128)(2,1)S(1)}, bf16[1,1024,512]{2,1,0:T(8,128)(2,1)}, u32[]{:S(2)}) copy-start(bf16[1,1024,512]{2,1,0:T(8,128)(2,1)} %param.7) | copy-start | bytes 3145732
Sparse Core Ops, SparseCore 0:
  18.3 47.2 reduce-scatter.1
where the time goes:
time: 207 us; the launch traced here: 206 us
  matrix products  48.8 us (24%)
  waiting for transfers between devices  46 us (22%)
  blocking collectives  37.1 us (18%)
  local copies, waits for them, and re-layouts  34.2 us (17%)
  other arithmetic  24.9 us (12%)
  between operations  14.9 us (7%)
    reduce_scatter x1, waiting for transfers between devices, shards(): lax.psum_scatter(lax.dot_general(tokens_here, grads_here, (((0,), (0,)),...  45.9 us
    all_gather x1, blocking collectives, shards(): pieces = lax.all_gather(shaped, 'replica', axis=0, tiled=True)  30.6 us
    dot_general x2, matrix products, inverse_tiled(): left = jnp.einsum('ka,ijkl->ijal', cosine, blocks, precision=highest)  12.5 us
    dot_general x2, matrix products, inverse_tiled(): jnp.einsum('ijal,lb->iajb', left, cosine, precision=highest)  12.2 us
    add x8, other arithmetic, add_one(): return total + band_mask(chosen) * values[:, :, None]  12.2 us
    dot_general x1, matrix products, shards(): lax.dot_general(tokens_here, grads_here, (((0,), (0,)), ((), ())), prefer...  9.75 us
    dot_general x1, matrix products, forward_tiled(): left = jnp.einsum('ka,iajb->ijkb', cosine, blocks, precision=highest)  9.44 us
    convert_element_type x2, local copies, waits for them, and re-layouts, shards(): update = (merged * scale_factor).astype(jnp.bfloat16)  8.17 us
  transfers between devices with their start and end apart: 1, of which 1 were waited for; matrix products, arithmetic and copies ran while one was open for 1% of the time, Pallas kernels for 0%

commit v1 on v0

v1 whole, which is shorter than its diff:
```python
import functools

import jax
import jax.numpy as jnp
import numpy as np
from jax import lax
from jax.experimental import pallas as pl
from jax.experimental.pallas import tpu as pltpu
from jax.sharding import PartitionSpec as P

TILE = 64
KEEP = 32
BAND = TILE * TILE // KEEP
GROUP = 256
PER = GROUP // TILE
BETA = 0.999
EPS = 1e-06

bf16 = jnp.bfloat16
f32 = jnp.float32
MIB = 1 << 20
VMEM = pl.BlockSpec(memory_space=pltpu.VMEM)
SMEM = pl.BlockSpec(memory_space=pltpu.SMEM)
HBM = pl.BlockSpec(memory_space=pltpu.HBM)
LANES = 128
SUBLANES = 8

FIRST_MIB = 56


def cosine_table():
    n = np.arange(TILE, dtype=np.float64)
    table = np.cos(np.pi * (2.0 * n[None, :] + 1.0) * n[:, None] / (2.0 * TILE))
    return table * np.where(n[:, None] == 0, np.sqrt(1.0 / TILE), np.sqrt(2.0 / TILE))


def halves(matrix):
    high = matrix.astype(np.float32).astype(bf16)
    low = (matrix - np.asarray(high, np.float64)).astype(np.float32).astype(bf16)
    return np.stack([high, low])


def tables():
    cosine = cosine_table()
    order = np.concatenate([np.arange(0, TILE, 2), np.arange(1, TILE, 2)])
    rows = np.kron(np.eye(PER), cosine)
    cols = np.kron(np.eye(PER), cosine[order].T)
    return halves(rows), halves(cols), halves(rows.T.copy())


def split(x):
    high = x.astype(bf16)
    return high, (x - high.astype(f32)).astype(bf16)


def mdot(a, b):
    return jnp.dot(a, b, preferred_element_type=f32)


def ndot(a, b):
    return lax.dot_general(a, b, (((1,), (1,)), ((), ())), preferred_element_type=f32)


def product(dot, a, b):
    out = dot(a[0], b[0]) + dot(a[1], b[0])
    return out if len(b) == 1 else out + dot(a[0], b[1])


def forward_group(x, rows, cols):
    high, low = split(product(ndot, rows, x))
    return mdot(high, cols[0]) + mdot(low, cols[0]) + mdot(high, cols[1])


def inverse_group(spectrum, rows_t, cols):
    return product(ndot, cols, split(product(mdot, rows_t, split(spectrum))))


def lane_block(shape):
    return lax.broadcasted_iota(jnp.int32, shape, len(shape) - 1) // KEEP


def offset_rows(index):
    value = (index & (BAND - 1)).astype(f32)
    value = jnp.concatenate([value] * (LANES // KEEP), axis=0).T
    value = value.reshape(-1, 2, SUBLANES, LANES)
    block = lane_block((value.shape[0], SUBLANES, LANES))
    return jnp.where(block < 2, value[:, 0], value[:, 1]) - jnp.where(block % 2 == 1, float(TILE), 0.0)


def packed(rows):
    rows = rows.reshape(-1, 2, SUBLANES, LANES)
    even, odd = rows[:, 0], rows[:, 1]
    axis = even.ndim - 1
    even = even + pltpu.roll(even, KEEP, axis)
    odd = odd + pltpu.roll(odd, KEEP, axis)
    return jnp.where(lane_block(even.shape) % 2 == 1, even, pltpu.roll(odd, LANES - KEEP, axis))


def unpacked(rows):
    axis = rows.ndim - 1
    upper = lane_block(rows.shape) % 2 == 1
    even = jnp.where(upper, rows, pltpu.roll(rows, LANES - KEEP, axis))
    odd = jnp.where(upper, pltpu.roll(rows, KEEP, axis), rows)
    return even, odd


def row_iota():
    return lax.broadcasted_iota(jnp.int32, (TILE, LANES), 0).astype(f32)


def params(mib):
    return pltpu.CompilerParams(vmem_limit_bytes=mib * MIB)


def cost(flops, bytes_accessed):
    return pl.CostEstimate(flops=flops, bytes_accessed=bytes_accessed, transcendentals=0)


def outer(a, c):
    return lax.dot_general(a, c, (((0,), (0,)), ((), ())), preferred_element_type=f32)


def first_kernel(mine, a_ref, c_ref, o_ref, far, tokens, far_sem, c_sem):
    half = o_ref.shape[0] // 2
    start = (mine[0] ^ 3) * o_ref.shape[0]
    cotangents = pltpu.make_async_copy(c_ref, tokens, c_sem)
    parts = [
        pltpu.make_async_copy(
            a_ref.at[:, pl.ds(pl.multiple_of(start + i * half, LANES), half)], far.at[i], far_sem.at[i]
        )
        for i in range(2)
    ]
    for copy in [cotangents] + parts:
        copy.start()
    cotangents.wait()
    for i, copy in enumerate(parts):
        copy.wait()
        o_ref[i * half : (i + 1) * half, :] = outer(far[i], tokens[...]).astype(bf16)


def first_product(mine, activations, cotangents, rows):
    tokens, kv = cotangents.shape
    return pl.pallas_call(
        first_kernel,
        in_specs=[SMEM, HBM, HBM],
        out_specs=VMEM,
        out_shape=jax.ShapeDtypeStruct((rows, kv), bf16),
        scratch_shapes=[
            pltpu.VMEM((2, tokens, rows // 2), bf16),
            pltpu.VMEM((tokens, kv), bf16),
            pltpu.SemaphoreType.DMA((2,)),
            pltpu.SemaphoreType.DMA,
        ],
        compiler_params=params(FIRST_MIB),
        cost_estimate=cost(2 * tokens * rows * kv, tokens * rows * 2),
        name="first_product",
    )(mine, activations, cotangents)


def product_kernel(distance, mine, a_ref, c_ref, o_ref):
    half = o_ref.shape[0] // 2
    start = (mine[0] ^ distance) * o_ref.shape[0]
    for i in range(2):
        columns = pl.ds(pl.multiple_of(start + i * half, LANES), half)
        o_ref[i * half : (i + 1) * half, :] = outer(a_ref[:, columns], c_ref[...]).astype(o_ref.dtype)


def held_product(distance, mine, activations, cotangents, rows, dtype):
    tokens, kv = cotangents.shape
    return pl.pallas_call(
        functools.partial(product_kernel, distance),
        in_specs=[SMEM, VMEM, VMEM],
        out_specs=VMEM,
        out_shape=jax.ShapeDtypeStruct((rows, kv), dtype),
        compiler_params=params(12),
        cost_estimate=cost(2 * tokens * rows * kv, tokens * rows * 2),
        name="held_product",
    )(mine, activations, cotangents)


def add_kernel(x_ref, y_ref, *o_refs):
    row = 0
    for o_ref in o_refs:
        end = row + o_ref.shape[0]
        o_ref[...] = (x_ref[row:end, :] + y_ref[row:end, :].astype(f32)).astype(bf16)
        row = end


def add_round(x, y, pieces):
    rows, kv = x.shape
    return pl.pallas_call(
        add_kernel,
        in_specs=[VMEM, VMEM],
        out_specs=[VMEM] * len(pieces),
        out_shape=[jax.ShapeDtypeStruct((n, kv), bf16) for n in pieces],
        compiler_params=params(4),
        cost_estimate=cost(rows * kv * 400, rows * kv * 8),
        name="chip_sum",
    )(x, y)


def pick(spectrum, row, col, offset_ref, rows_ref):
    line = row_iota()
    for pair in range(GROUP // LANES):
        for tile in range(PER):
            at = (row // LANES + pair) * SUBLANES + col // TILE + tile
            part = spectrum[tile * TILE : (tile + 1) * TILE, pair * LANES : (pair + 1) * LANES]
            part = jnp.where(offset_ref[at : at + 1, :] == line, part, 0.0)
            rows_ref[at : at + 1, :] = jnp.sum(part, axis=0, keepdims=True)


def kept_cross_kernel(index_ref, row_ref, col_ref, *refs):
    *x_refs, o_ref, offset_ref, rows_ref = refs
    offset_ref[...] = offset_rows(index_ref[...]).reshape(offset_ref.shape)
    first = 0
    for x_ref in x_refs:
        for row in range(0, x_ref.shape[0], GROUP):
            for col in range(0, x_ref.shape[1], GROUP):
                x = x_ref[row : row + GROUP, col : col + GROUP]
                pick(forward_group((x,), row_ref, col_ref), first + row, col, offset_ref, rows_ref)
        first += x_ref.shape[0]
    o_ref[...] = packed(rows_ref[...]).reshape(o_ref.shape)


def row_scratch(tiles, count=None):
    shape = (tiles // 2, LANES)
    return pltpu.VMEM(shape if count is None else (count, *shape), f32)


def kept_cross(pieces, index, rows, cols):
    tiles = index.shape[1]
    return pl.pallas_call(
        kept_cross_kernel,
        in_specs=[VMEM] * (3 + len(pieces)),
        out_specs=VMEM,
        out_shape=jax.ShapeDtypeStruct((tiles // 4, LANES), f32),
        scratch_shapes=[row_scratch(tiles), row_scratch(tiles)],
        compiler_params=params(8),
        cost_estimate=cost(2 * 10**9, MIB),
        name="kept_cross",
    )(index, rows, cols, *pieces)


def kept_own_kernel(x_ref, y_ref, momentum_ref, index_ref, cross_ref, row_ref, col_ref, moment_ref, o_ref, offset_ref, rows_ref):
    offset_ref[...] = offset_rows(index_ref[...]).reshape(offset_ref.shape)
    for row in range(0, x_ref.shape[0], GROUP):
        for col in range(0, x_ref.shape[1], GROUP):
            at = (slice(row, row + GROUP), slice(col, col + GROUP))
            x = x_ref[at] + y_ref[at].astype(f32) + BETA * momentum_ref[at]
            moment_ref[at] = x
            pick(forward_group(split(x), row_ref, col_ref), row, col, offset_ref, rows_ref)
    o_ref[...] = cross_ref[...] + packed(rows_ref[...]).reshape(o_ref.shape)


def kept_own(partial, received, momentum, index, cross, rows, cols):
    tiles = index.shape[1]
    return pl.pallas_call(
        kept_own_kernel,
        in_specs=[VMEM] * 7,
        out_specs=[VMEM, VMEM],
        out_shape=[jax.ShapeDtypeStruct(partial.shape, f32), jax.ShapeDtypeStruct(cross.shape, f32)],
        scratch_shapes=[row_scratch(tiles), row_scratch(tiles)],
        compiler_params=params(8),
        cost_estimate=cost(2 * 10**9, 4 * MIB),
        name="kept_own",
    )(partial, received, momentum, index, cross, rows, cols)


def store_unpacked(packed_rows, to_ref):
    rows = packed_rows.reshape(-1, SUBLANES, LANES)
    even, odd = unpacked(rows)
    for i in range(rows.shape[0]):
        to_ref[2 * i * SUBLANES : (2 * i + 1) * SUBLANES, :] = even[i]
        to_ref[(2 * i + 1) * SUBLANES : (2 * i + 2) * SUBLANES, :] = odd[i]


def drop_sent_kernel(moment_ref, kept_ref, index_ref, row_t_ref, col_ref, o_ref, offset_ref, value_ref):
    offset_ref[...] = offset_rows(index_ref[...]).reshape(offset_ref.shape)
    store_unpacked(kept_ref[...], value_ref)
    line = row_iota()
    for row in range(0, moment_ref.shape[0], GROUP):
        for col in range(0, moment_ref.shape[1], GROUP):
            lanes = []
            for pair in range(GROUP // LANES):
                first = (row // LANES + pair) * SUBLANES + col // TILE
                lanes.append(
                    jnp.concatenate(
                        [
                            jnp.where(offset_ref[i : i + 1, :] == line, value_ref[i : i + 1, :], 0.0)
                            for i in range(first, first + PER)
                        ],
                        axis=0,
                    )
                )
            at = (slice(row, row + GROUP), slice(col, col + GROUP))
            o_ref[at] = moment_ref[at] - inverse_group(jnp.concatenate(lanes, axis=1), row_t_ref, col_ref)


def drop_sent(moment, kept, index, rows_t, cols):
    tiles = index.shape[1]
    return pl.pallas_call(
        drop_sent_kernel,
        in_specs=[VMEM] * 5,
        out_specs=VMEM,
        out_shape=jax.ShapeDtypeStruct(moment.shape, f32),
        scratch_shapes=[row_scratch(tiles), row_scratch(tiles)],
        compiler_params=params(8),
        cost_estimate=cost(2 * 10**9, 4 * MIB),
        name="drop_sent",
    )(moment, kept, index, rows_t, cols)


def sum_kernel(counts, me_ref, index_ref, *refs):
    *kept_refs, o_ref, square_ref, offset_ref, value_ref = refs
    replicas = sum(counts)
    slot = 0
    for kept_ref, count in zip(kept_refs, counts):
        for i in range(count):
            index = index_ref[me_ref[0] ^ slot]
            offset_ref[slot] = offset_rows(index).reshape(offset_ref.shape[1:])
            store_unpacked(kept_ref[i], value_ref.at[slot])
            slot += 1
    line = row_iota()
    squares = jnp.zeros((TILE, LANES), f32)
    for pair in range(o_ref.shape[1] // LANES):
        for tile in range(o_ref.shape[0] // TILE):
            at = pair * SUBLANES + tile

            def add(slot, total):
                return total + jnp.where(
                    offset_ref[slot, at : at + 1, :] == line, value_ref[slot, at : at + 1, :], 0.0
                )

            total = lax.fori_loop(0, replicas, add, jnp.zeros((TILE, LANES), f32), unroll=min(replicas, 8))
            o_ref[tile * TILE : (tile + 1) * TILE, pair * LANES : (pair + 1) * LANES] = total
            squares += total * total
    total = jnp.sum(squares, axis=0, keepdims=True)
    square_ref[...] = jnp.broadcast_to(jnp.sum(total, axis=1, keepdims=True), square_ref.shape)


def sum_replicas(me, index, pieces, rows, kv):
    tiles = index.shape[2]
    counts = [piece.shape[0] for piece in pieces]
    return pl.pallas_call(
        functools.partial(sum_kernel, counts),
        in_specs=[SMEM] + [VMEM] * (1 + len(pieces)),
        out_specs=[VMEM, VMEM],
        out_shape=[jax.ShapeDtypeStruct((kv, rows), f32), jax.ShapeDtypeStruct((SUBLANES, LANES), f32)],
        scratch_shapes=[row_scratch(tiles, sum(counts)), row_scratch(tiles, sum(counts))],
        compiler_params=params(12),
        cost_estimate=cost(3 * 10**9, 4 * MIB),
        name="sum_replicas",
    )(me, index, *pieces)


def inverse_kernel(x_ref, row_t_ref, col_ref, o_ref):
    for row in range(0, o_ref.shape[0], GROUP):
        for col in range(0, o_ref.shape[1], GROUP):
            at = (slice(row, row + GROUP), slice(col, col + GROUP))
            o_ref[at] = inverse_group(x_ref[at[1], at[0]], row_t_ref, col_ref)


def inverse(x, rows_t, cols):
    return pl.pallas_call(
        inverse_kernel,
        in_specs=[VMEM] * 3,
        out_specs=VMEM,
        out_shape=jax.ShapeDtypeStruct(x.shape[::-1], f32),
        compiler_params=params(8),
        cost_estimate=cost(2 * 10**9, 4 * MIB),
        name="inverse",
    )(x, rows_t, cols)


def update_kernel(factor, divisor, merged_ref, square_ref, o_ref):
    scale = lax.rsqrt(square_ref[0:1, 0:1] * factor + EPS) * divisor
    o_ref[...] = (merged_ref[...] * scale).astype(o_ref.dtype)


def scaled(merged, squares, factor, divisor):
    return pl.pallas_call(
        functools.partial(update_kernel, factor, divisor),
        in_specs=[VMEM, VMEM],
        out_specs=VMEM,
        out_shape=jax.ShapeDtypeStruct(merged.shape, bf16),
        compiler_params=params(8),
        cost_estimate=cost(10**7, 4 * MIB),
        name="scaled",
    )(merged, squares)


def shards(replicas, shards_count, activations, cotangents, momentum, keep_index):
    activations, cotangents, momentum = activations[0], cotangents[0], momentum[0]
    rows, kv = momentum.shape
    rows_f, cols_f, rows_t = (jnp.asarray(t) for t in tables())

    mine = lax.axis_index("fsdp").astype(jnp.int32).reshape(1)
    replica = lax.axis_index("replica")
    near = [(i, i ^ 1) for i in range(shards_count)]
    cross = [(i, i ^ 2) for i in range(shards_count)]

    index = keep_index.transpose(0, 2, 1)
    own_index = lax.dynamic_index_in_dim(index, replica, 0, keepdims=False)

    part = first_product(mine, activations, cotangents, rows)
    cross_index = lax.ppermute(own_index, "fsdp", cross)
    got = lax.ppermute(part, "fsdp", near)
    part = held_product(2, mine, activations, cotangents, rows, f32)
    first, second = add_round(part, got, (GROUP, rows - GROUP))
    bulk_first = lax.ppermute(first, "fsdp", cross)
    cross_kept = kept_cross((first, second), cross_index, rows_f, cols_f)
    second, cross_kept = lax.optimization_barrier((second, cross_kept))
    cross_kept = lax.ppermute(cross_kept, "fsdp", cross)
    bulk_second = lax.ppermute(second, "fsdp", cross)

    part = held_product(1, mine, activations, cotangents, rows, bf16)
    got = lax.ppermute(part, "fsdp", near)
    part = held_product(0, mine, activations, cotangents, rows, f32)
    moment, kept = kept_own(part, got, momentum, own_index, cross_kept, rows_f, cols_f)

    pieces = [kept[None]]
    bit = 1
    while bit < replicas:
        held = pieces[0] if len(pieces) == 1 else jnp.concatenate(pieces)
        shifts = [bit] if bit == 1 or 2 * bit >= replicas else [bit, 2 * bit, 3 * bit]
        pieces = [held] + [lax.ppermute(held, "replica", [(i, i ^ shift) for i in range(replicas)]) for shift in shifts]
        bit *= len(shifts) + 1

    remaining = drop_sent(moment, kept, own_index, rows_t, cols_f)
    summed, squares = sum_replicas(replica.astype(jnp.int32).reshape(1), index, pieces, rows, kv)
    squares = squares + lax.ppermute(squares, "fsdp", near)
    squares = squares + lax.ppermute(squares, "fsdp", cross)
    merged = inverse(summed, rows_t, cols_f)
    count = float(shards_count * rows * kv) * float(replicas) ** 2
    update = scaled(merged, squares, 1.0 / count, 1.0 / replicas)
    new_momentum = remaining + jnp.concatenate([bulk_first, bulk_second]).astype(f32)
    return new_momentum[None], update


def solution(mesh):
    in_specs = (
        P("replica", "fsdp", None),
        P("replica", "fsdp", None),
        P("replica", "fsdp", None),
        P(None, "fsdp", None),
    )
    out_specs = (P("replica", "fsdp", None), P("fsdp", None))
    body = functools.partial(shards, mesh.shape["replica"], mesh.shape["fsdp"])
    return jax.shard_map(body, mesh=mesh, in_specs=in_specs, out_specs=out_specs, check_vma=False)
```

time: 207 us -> 56.8 us (0.27)
  matrix products: 48.8 us -> 0 us
  blocking collectives: 37.1 us -> 0 us
  waiting for transfers between devices: 46 us -> 12.9 us
  local copies, waits for them, and re-layouts: 34.2 us -> 7.57 us
  other arithmetic: 24.9 us -> 1.71 us
  Pallas kernels: 0 us -> 22.6 us
  between operations: 14.9 us -> 0.79 us
  starting transfers between devices: 0.04 us -> 10.9 us
    dot_general x7 -> x0, matrix products: 48.8 us -> none  [the longest x2 12.5 us: inverse_tiled(): left = jnp.einsum('ka,ijkl->ijal', cosine, blocks, precision=highest)]
    reduce_scatter x1 -> x0, waiting for transfers between devices: 45.9 us -> none  [shards(): lax.psum_scatter(lax.dot_general(tokens_here, grads_here, (((0,), (0,)),...]
    all_gather x1 -> x0, blocking collectives: 30.6 us -> none  [shards(): pieces = lax.all_gather(shaped, 'replica', axis=0, tiled=True)]
    pallas_call x0 -> x11, Pallas kernels: none -> 22.6 us  [the longest x1 4.14 us: first_product(): pl.pallas_call(first_kernel, in_specs=[SMEM, HBM, HBM], out_specs=VMEM, o...]
    add x9 -> x2, other arithmetic: 15.8 us -> 0.01 us  [the longest x1 0.01 us: shards(): squares = squares + lax.ppermute(squares, 'fsdp', near)]
    ppermute x0 -> x12, waiting for transfers between devices: none -> 12.9 us  [the longest x4 5.46 us: shards(): lax.ppermute(held, 'replica', [(i, i ^ shift) for i in range(replicas)])]
    reshape x3 -> x0, local copies, waits for them, and re-layouts: 11.5 us -> none  [the longest x1 4.79 us: inverse_tiled(): jnp.einsum('ijal,lb->iajb', left, cosine, precision=highest)]
    ppermute x0 -> x12, starting transfers between devices: none -> 10.9 us  [the longest x4 5.92 us: shards(): lax.ppermute(held, 'replica', [(i, i ^ shift) for i in range(replicas)])]
  transfers between devices with their start and end apart: 1 -> 12, of which waited for: 1 -> 5; matrix products, arithmetic and copies ran while one was open for 1% -> 0% of each run, Pallas kernels for 0% -> 26%
where the time goes in v1:
time: 56.8 us; the launch traced here: 56.5 us
  Pallas kernels  22.6 us (40%)
  waiting for transfers between devices  12.9 us (23%)
  starting transfers between devices  10.9 us (19%)
  local copies, waits for them, and re-layouts  7.57 us (13%)
  other arithmetic  1.71 us (3%)
  between operations  0.79 us (1%)
    unnamed x16, local copies, waits for them, and re-layouts  7.56 us
    ppermute x4, starting transfers between devices, shards(): lax.ppermute(held, 'replica', [(i, i ^ shift) for i in range(replicas)])  5.92 us
    ppermute x4, waiting for transfers between devices, shards(): lax.ppermute(held, 'replica', [(i, i ^ shift) for i in range(replicas)])  5.46 us
    ppermute x1, waiting for transfers between devices, shards(): squares = squares + lax.ppermute(squares, 'fsdp', cross)  5.02 us
    pallas_call x1, Pallas kernels, first_product(): pl.pallas_call(first_kernel, in_specs=[SMEM, HBM, HBM], out_specs=VMEM, o...  4.14 us
    pallas_call x3, Pallas kernels, held_product(): pl.pallas_call(functools.partial(product_kernel, distance), in_specs=[SME...  3.95 us
    pallas_call x1, Pallas kernels, kept_own(): pl.pallas_call(kept_own_kernel, in_specs=[VMEM] * 7, out_specs=[VMEM, VME...  3.9 us
    ppermute x1, starting transfers between devices, shards(): cross_index = lax.ppermute(own_index, 'fsdp', cross)  2.96 us
  transfers between devices with their start and end apart: 12, of which 5 were waited for; matrix products, arithmetic and copies ran while one was open for 0% of the time, Pallas kernels for 26%

profile of v1, /device:TPU:0, one launch (start us, length us, event | category | flops | bytes accessed | tf_op | source)
XLA Modules:
  0.0 56.5 jit_solution(1540183932423206574)
XLA Ops:
  0.6 0.0 copy-start.2
  0.6 4.1 %first_product.1 = bf16[1024,512]{1,0:T(8,128)(2,1)} custom-call(s32[1]{0:T(128)} %bitcast.mine, bf16[1024,4096]{1,0:T(8,128)(2,1)} %bitcast.13, bf16[1024,512]{1,0:T(8,128)(2,1)} %bitcast.17), custom_call_target="tpu_custom_call" | custom-call | flops 1073741824 | bytes 2097152 | tf_op jit(solution)/shard_map/first_product/pallas_call | solution.py:143
  4.8 0.6 %collective-permute-start.1 = (bf16[1024,512]{1,0:T(8,128)(2,1)}, bf16[1024,512]{1,0:T(8,128)(2,1)S(1)}, u32[]{:S(2)}, u32[]{:S(2)}) collective-permute-start(bf16[1024,512]{1,0:T(8,128)(2,1)} %first_product.1), channel_id=1, source_target_pairs={{0,1},{1,0},{2,3},{3,2},{4,5},{5,4},{6,7},{7,6},{8,9},{9,8},{10,11... | collective-permute-start | bytes 3145736 | tf_op jit(solution)/shard_map/ppermute | solution.py:407
  5.4 0.0 copy-done.2
  5.4 0.0 copy-start
  5.4 3.4 %copy-done = bf16[1,1024,4096]{2,1,0:T(8,128)(2,1)S(1)} copy-done((bf16[1,1024,4096]{2,1,0:T(8,128)(2,1)S(1)}, bf16[1,1024,4096]{2,1,0:T(8,128)(2,1)}, u32[]{:S(2)}) %copy-start) | copy-done | bytes 8388632
  8.8 0.0 copy-start.3
  8.8 1.3 %held_product.4 = bf16[1024,512]{1,0:T(8,128)(2,1)S(1)} custom-call(s32[1]{0:T(128)} %bitcast.mine, bf16[1024,4096]{1,0:T(8,128)(2,1)S(1)} %bitcast.14, bf16[1024,512]{1,0:T(8,128)(2,1)S(1)} %bitcast.18), custom_call_target="tpu_custom_call" | custom-call | flops 1073741824 | bytes 2097152 | tf_op jit(solution)/shard_map/held_product/pallas_call | solution.py:170
  10.1 0.1 collective-permute-start
  10.2 0.0 copy-done.3
  10.2 3.0 %collective-permute-start.2 = (s32[32,128]{1,0:T(8,128)S(1)}, s32[32,128]{1,0:T(8,128)S(1)}, u32[]{:S(2)}, u32[]{:S(2)}) collective-permute-start(s32[32,128]{1,0:T(8,128)S(1)} %dynamic-slice_bitcast_fusion.index_ref), channel_id=1, source_target_pairs={{0,2},{1,3},{2,0},{3,1},{4,6},{5,7},{6,4},{7,5},{8,10},{9,11},{10,... | collective-permute-start | bytes 49160 | tf_op jit(solution)/shard_map/ppermute | solution.py:406
  13.2 0.0 copy-start.1
  13.2 3.4 %copy-done.1 = bf16[1,1024,4096]{2,1,0:T(8,128)(2,1)S(1)} copy-done((bf16[1,1024,4096]{2,1,0:T(8,128)(2,1)S(1)}, bf16[1,1024,4096]{2,1,0:T(8,128)(2,1)}, u32[]{:S(2)}) %copy-start.1) | copy-done | bytes 8388632
  16.5 1.3 %held_product.5.x_ref = f32[1024,512]{1,0:T(8,128)S(1)} custom-call(s32[1]{0:T(128)} %bitcast.mine, bf16[1024,4096]{1,0:T(8,128)(2,1)S(1)} %bitcast.15, bf16[1024,512]{1,0:T(8,128)(2,1)S(1)} %bitcast.19), custom_call_target="tpu_custom_call" | custom-call | flops 1073741824 | bytes 2097152 | tf_op jit(solution)/shard_map/held_product/pallas_call | solution.py:170
  17.9 0.0 copy-start.5
  17.9 0.0 copy-start.7
  17.9 0.0 collective-permute-done.1.y_ref
  17.9 0.2 chip_sum.1
  18.1 0.0 collective-permute-done.2.index_ref
  18.1 0.7 %copy-done.5 = bf16[2,256,256]{2,1,0:T(8,128)(2,1)S(1)} copy-done((bf16[2,256,256]{2,1,0:T(8,128)(2,1)S(1)}, bf16[2,256,256]{2,1,0:T(8,128)(2,1)}, u32[]{:S(2)}) %copy-start.5) | copy-done | bytes 262168
  18.8 0.1 copy-done.7
  18.9 1.9 %kept_cross.1 = f32[32,128]{1,0:T(8,128)S(1)} custom-call(s32[32,128]{1,0:T(8,128)S(1)} %collective-permute-done.2.index_ref, bf16[2,256,256]{2,1,0:T(8,128)(2,1)S(1)} %copy-done.7, bf16[2,256,256]{2,1,0:T(8,128)(2,1)S(1)} %copy-done.5, bf16[256,512]{1,0:T(8,128)(2,1)S(1)} %get-tuple-element.11.refs_0_, bf16[768,512]{1,0:T(8,128)(2,1)S(1)} %get-tuple-element.15.refs_1_), custom_call_target="tpu_custom_call" | custom-call | flops 2000000000 | bytes 1048576 | tf_op jit(solution)/shard_map/kept_cross/pallas_call | solution.py:232
  20.8 0.0 copy-start.4
  20.8 0.0 collective-permute-start.3
  20.9 1.3 %held_product.3.x_ref = f32[1024,512]{1,0:T(8,128)S(1)} custom-call(s32[1]{0:T(128)} %bitcast.mine, bf16[1024,4096]{1,0:T(8,128)(2,1)S(1)} %bitcast.16, bf16[1024,512]{1,0:T(8,128)(2,1)S(1)} %bitcast.20), custom_call_target="tpu_custom_call" | custom-call | flops 1073741824 | bytes 2097152 | tf_op jit(solution)/shard_map/held_product/pallas_call | solution.py:170
  22.2 0.0 collective-permute-done.y_ref
  22.2 2.4 %collective-permute-done.3.cross_ref = f32[32,128]{1,0:T(8,128)S(1)} collective-permute-done((f32[32,128]{1,0:T(8,128)S(1)}, f32[32,128]{1,0:T(8,128)S(1)}, u32[]{:S(2)}, u32[]{:S(2)}) %collective-permute-start.3) | collective-permute-done | bytes 16416 | tf_op jit(solution)/shard_map/ppermute | solution.py:413
  24.6 0.0 copy-done.4
  24.6 3.9 %kept_own.1 = (f32[1024,512]{1,0:T(8,128)S(1)}, f32[32,128]{1,0:T(8,128)S(1)}) custom-call(f32[1024,512]{1,0:T(8,128)S(1)} %held_product.3.x_ref, bf16[1024,512]{1,0:T(8,128)(2,1)} %collective-permute-done.y_ref, f32[1024,512]{1,0:T(8,128)S(1)} %bitcast.24, s32[32,128]{1,0:T(8,128)S(1)} %dynamic-slice_bitcast_fusion.index_ref, ...), custom_call_target="tpu_custom_call" | custom-call | flops 2000000000 | bytes 4194304 | tf_op jit(solution)/shard_map/kept_own/pallas_call | solution.py:257
  28.5 1.5 %collective-permute-start.6 = (f32[1,32,128]{2,1,0:T(8,128)S(1)}, f32[1,32,128]{2,1,0:T(8,128)S(1)}, u32[]{:S(2)}, u32[]{:S(2)}) collective-permute-start(f32[1,32,128]{2,1,0:T(8,128)S(1)} %bitcast.21), channel_id=1, source_target_pairs={{0,4},{4,0},{8,12},{12,8},{16,20},{20,16},{24,28},{28,24},{1,5},{5... | collective-permute-start | bytes 49160 | tf_op jit(solution)/shard_map/ppermute | solution.py:426
  30.0 0.5 collective-permute-start.5
  30.6 1.7 %collective-permute-done.6 = f32[1,32,128]{2,1,0:T(8,128)S(1)} collective-permute-done((f32[1,32,128]{2,1,0:T(8,128)S(1)}, f32[1,32,128]{2,1,0:T(8,128)S(1)}, u32[]{:S(2)}, u32[]{:S(2)}) %collective-permute-start.6) | collective-permute-done | bytes 16416 | tf_op jit(solution)/shard_map/ppermute | solution.py:426
  32.3 3.6 %collective-permute-start.9 = (f32[2,32,128]{2,1,0:T(8,128)S(1)}, f32[2,32,128]{2,1,0:T(8,128)S(1)}, u32[]{:S(2)}, u32[]{:S(2)}) collective-permute-start(f32[2,32,128]{2,1,0:T(8,128)S(1)} %pad_maximum_fusion.refs_0_), channel_id=1, source_target_pairs={{0,24},{4,28},{8,16},{12,20},{16,8},{20,12},{24,0},{28,4},{1,25},{... | collective-permute-start | bytes 98312 | tf_op jit(solution)/shard_map/ppermute | solution.py:426
  35.9 0.0 collective-permute-start.8
  35.9 0.8 %collective-permute-start.7 = (f32[2,32,128]{2,1,0:T(8,128)S(1)}, f32[2,32,128]{2,1,0:T(8,128)S(1)}, u32[]{:S(2)}, u32[]{:S(2)}) collective-permute-start(f32[2,32,128]{2,1,0:T(8,128)S(1)} %pad_maximum_fusion.refs_0_), channel_id=1, source_target_pairs={{0,8},{4,12},{8,0},{12,4},{16,24},{20,28},{24,16},{28,20},{1,9},{5... | collective-permute-start | bytes 98312 | tf_op jit(solution)/shard_map/ppermute | solution.py:426
  36.7 0.3 collective-permute-start.4
  36.9 1.2 %collective-permute-done.9.refs_3_ = f32[2,32,128]{2,1,0:T(8,128)S(1)} collective-permute-done((f32[2,32,128]{2,1,0:T(8,128)S(1)}, f32[2,32,128]{2,1,0:T(8,128)S(1)}, u32[]{:S(2)}, u32[]{:S(2)}) %collective-permute-start.9) | collective-permute-done | bytes 32800 | tf_op jit(solution)/shard_map/ppermute | solution.py:426
  38.2 2.5 %collective-permute-done.8.refs_2_ = f32[2,32,128]{2,1,0:T(8,128)S(1)} collective-permute-done((f32[2,32,128]{2,1,0:T(8,128)S(1)}, f32[2,32,128]{2,1,0:T(8,128)S(1)}, u32[]{:S(2)}, u32[]{:S(2)}) %collective-permute-start.8) | collective-permute-done | bytes 32800 | tf_op jit(solution)/shard_map/ppermute | solution.py:426
  40.7 0.0 collective-permute-done.7.refs_1_
  40.7 0.0 copy-start.6
  40.7 2.4 %sum_replicas.1 = (f32[512,1024]{1,0:T(8,128)S(1)}, f32[8,128]{1,0:T(8,128)S(1)}) custom-call(s32[1]{0:T(128)} %bitcast.8.me_ref, s32[8,32,128]{2,1,0:T(8,128)S(1)} %bitcast.23, f32[2,32,128]{2,1,0:T(8,128)S(1)} %pad_maximum_fusion.refs_0_, f32[2,32,128]{2,1,0:T(8,128)S(1)} %collective-permute-done.7.refs_1_, ...), custom_call_target="tpu_custom_call" | custom-call | flops 3000000000 | bytes 4194304 | tf_op jit(solution)/shard_map/sum_replicas/pallas_call | solution.py:344
  43.1 0.0 collective-permute-start.10
  43.1 0.0 copy-done.6
  43.1 2.7 %drop_sent.1 = f32[1024,512]{1,0:T(8,128)S(1)} custom-call(f32[1024,512]{1,0:T(8,128)S(1)} %get-tuple-element.13.moment_ref, f32[32,128]{1,0:T(8,128)S(1)} %get-tuple-element.14.kept_ref, s32[32,128]{1,0:T(8,128)S(1)} %dynamic-slice_bitcast_fusion.index_ref, bf16[2,256,256]{2,1,0:T(8,128)(2,1)S(1)} %copy-done.6, bf16[2,256,256]{2,1,0:T(8,128)(2,1)S(1)} %copy-done.5), custom_call_target="tpu_custom_call" | custom-call | flops 2000000000 | bytes 4194304 | tf_op jit(solution)/shard_map/drop_sent/pallas_call | solution.py:301
  45.8 0.0 collective-permute-done.10
  45.9 0.6 %collective-permute-start.11 = (f32[8,128]{1,0:T(8,128)S(1)}, f32[8,128]{1,0:T(8,128)S(1)}, u32[]{:S(2)}, u32[]{:S(2)}) collective-permute-start(f32[8,128]{1,0:T(8,128)S(1)} %add.15), channel_id=1, source_target_pairs={{0,2},{1,3},{2,0},{3,1},{4,6},{5,7},{6,4},{7,5},{8,10},{9,11},{10,... | collective-permute-start | bytes 12296 | tf_op jit(solution)/shard_map/ppermute | solution.py:432
  46.4 2.1 %inverse.1.merged_ref = f32[1024,512]{1,0:T(8,128)S(1)} custom-call(f32[512,1024]{1,0:T(8,128)S(1)} %get-tuple-element.16.x_ref, bf16[2,256,256]{2,1,0:T(8,128)(2,1)S(1)} %copy-done.6, bf16[2,256,256]{2,1,0:T(8,128)(2,1)S(1)} %copy-done.5), custom_call_target="tpu_custom_call" | custom-call | flops 2000000000 | bytes 4194304 | tf_op jit(solution)/shard_map/inverse/pallas_call | solution.py:364
  48.6 5.0 %collective-permute-done.11 = f32[8,128]{1,0:T(8,128)S(1)} collective-permute-done((f32[8,128]{1,0:T(8,128)S(1)}, f32[8,128]{1,0:T(8,128)S(1)}, u32[]{:S(2)}, u32[]{:S(2)}) %collective-permute-start.11) | collective-permute-done | bytes 4128 | tf_op jit(solution)/shard_map/ppermute | solution.py:432
  53.6 1.2 %scaled.1 = bf16[1024,512]{1,0:T(8,128)(2,1)} custom-call(f32[1024,512]{1,0:T(8,128)S(1)} %inverse.1.merged_ref, f32[8,128]{1,0:T(8,128)S(1)} %add.16.square_ref), custom_call_target="tpu_custom_call" | custom-call | flops 10000000 | bytes 4194304 | tf_op jit(solution)/shard_map/scaled/pallas_call | solution.py:381
  54.8 0.0 collective-permute-done.4
  54.8 0.0 collective-permute-done.5
  54.8 1.7 %add_bitcast_fusion = f32[1,1024,512]{2,1,0:T(8,128)} fusion(f32[1024,512]{1,0:T(8,128)S(1)} %drop_sent.1, bf16[768,512]{1,0:T(8,128)(2,1)S(1)} %collective-permute-done.5, bf16[256,512]{1,0:T(8,128)(2,1)S(1)} %collective-permute-done.4), kind=kLoop, calls=%fused_computation | loop fusion | flops 2621440 | bytes 5242880 | tf_op jit(solution)/shard_map/broadcast_in_dim | solution.py:437
  (4 shorter events, 0.0 us)
Async XLA Ops:
  0.6 4.7 %copy-start.2 = (bf16[1,1024,512]{2,1,0:T(8,128)(2,1)S(1)}, bf16[1,1024,512]{2,1,0:T(8,128)(2,1)}, u32[]{:S(2)}) copy-start(bf16[1,1024,512]{2,1,0:T(8,128)(2,1)} %param.8) | copy-start | bytes 3145732
  4.8 13.1 %collective-permute-start.1 = (bf16[1024,512]{1,0:T(8,128)(2,1)}, bf16[1024,512]{1,0:T(8,128)(2,1)S(1)}, u32[]{:S(2)}, u32[]{:S(2)}) collective-permute-start(bf16[1024,512]{1,0:T(8,128)(2,1)} %first_product.1), channel_id=1, source_target_pairs={{0,1},{1,0},{2,3},{3,2},{4,5},{5,4},{6,7},{7,6},{8,9},{9,8},{10,11... | collective-permute-start | bytes 3145736 | tf_op jit(solution)/shard_map/ppermute | solution.py:407
  5.4 3.4 %copy-start = (bf16[1,1024,4096]{2,1,0:T(8,128)(2,1)S(1)}, bf16[1,1024,4096]{2,1,0:T(8,128)(2,1)}, u32[]{:S(2)}) copy-start(bf16[1,1024,4096]{2,1,0:T(8,128)(2,1)} %param.7) | copy-start | bytes 25165828
  8.8 1.4 %copy-start.3 = (s32[8,128,32]{1,2,0:T(8,128)S(1)}, s32[8,128,32]{1,2,0:T(8,128)}, u32[]{:S(2)}) copy-start(s32[8,128,32]{1,2,0:T(8,128)} %param.10) | copy-start | bytes 393220
  10.1 12.1 %collective-permute-start = (bf16[1024,512]{1,0:T(8,128)(2,1)S(1)}, bf16[1024,512]{1,0:T(8,128)(2,1)}, u32[]{:S(2)}, u32[]{:S(2)}) collective-permute-start(bf16[1024,512]{1,0:T(8,128)(2,1)S(1)} %held_product.4), channel_id=1, source_target_pairs={{0,1},{1,0},{2,3},{3,2},{4,5},{5,4},{6,7},{7,6},{8,9},{9,8},{10,11... | collective-permute-start | bytes 3145736 | tf_op jit(solution)/shard_map/ppermute | solution.py:417
  10.2 7.9 %collective-permute-start.2 = (s32[32,128]{1,0:T(8,128)S(1)}, s32[32,128]{1,0:T(8,128)S(1)}, u32[]{:S(2)}, u32[]{:S(2)}) collective-permute-start(s32[32,128]{1,0:T(8,128)S(1)} %dynamic-slice_bitcast_fusion.index_ref), channel_id=1, source_target_pairs={{0,2},{1,3},{2,0},{3,1},{4,6},{5,7},{6,4},{7,5},{8,10},{9,11},{10,... | collective-permute-start | bytes 49160 | tf_op jit(solution)/shard_map/ppermute | solution.py:406
  13.2 3.4 %copy-start.1 = (bf16[1,1024,4096]{2,1,0:T(8,128)(2,1)S(1)}, bf16[1,1024,4096]{2,1,0:T(8,128)(2,1)}, u32[]{:S(2)}) copy-start(bf16[1,1024,4096]{2,1,0:T(8,128)(2,1)} %param.7) | copy-start | bytes 25165828
  17.9 1.0 %copy-start.5 = (bf16[2,256,256]{2,1,0:T(8,128)(2,1)S(1)}, bf16[2,256,256]{2,1,0:T(8,128)(2,1)}, u32[]{:S(2)}) copy-start(bf16[2,256,256]{2,1,0:T(8,128)(2,1)} %constant.22.clone.col_ref) | copy-start | bytes 786436
  17.9 1.0 %copy-start.7 = (bf16[2,256,256]{2,1,0:T(8,128)(2,1)S(1)}, bf16[2,256,256]{2,1,0:T(8,128)(2,1)}, u32[]{:S(2)}) copy-start(bf16[2,256,256]{2,1,0:T(8,128)(2,1)} %constant.21.clone.row_ref) | copy-start | bytes 786436
  20.8 3.8 %copy-start.4 = (f32[1,1024,512]{2,1,0:T(8,128)S(1)}, f32[1,1024,512]{2,1,0:T(8,128)}, u32[]{:S(2)}) copy-start(f32[1,1024,512]{2,1,0:T(8,128)} %param.9) | copy-start | bytes 6291460
  20.8 3.8 %collective-permute-start.3 = (f32[32,128]{1,0:T(8,128)S(1)}, f32[32,128]{1,0:T(8,128)S(1)}, u32[]{:S(2)}, u32[]{:S(2)}) collective-permute-start(f32[32,128]{1,0:T(8,128)S(1)} %kept_cross.1), channel_id=1, source_target_pairs={{0,2},{1,3},{2,0},{3,1},{4,6},{5,7},{6,4},{7,5},{8,10},{9,11},{10,... | collective-permute-start | bytes 49160 | tf_op jit(solution)/shard_map/ppermute | solution.py:413
  28.5 3.8 %collective-permute-start.6 = (f32[1,32,128]{2,1,0:T(8,128)S(1)}, f32[1,32,128]{2,1,0:T(8,128)S(1)}, u32[]{:S(2)}, u32[]{:S(2)}) collective-permute-start(f32[1,32,128]{2,1,0:T(8,128)S(1)} %bitcast.21), channel_id=1, source_target_pairs={{0,4},{4,0},{8,12},{12,8},{16,20},{20,16},{24,28},{28,24},{1,5},{5... | collective-permute-start | bytes 49160 | tf_op jit(solution)/shard_map/ppermute | solution.py:426
  30.0 24.8 %collective-permute-start.5 = (bf16[768,512]{1,0:T(8,128)(2,1)S(1)}, bf16[768,512]{1,0:T(8,128)(2,1)S(1)}, u32[]{:S(2)}, u32[]{:S(2)}) collective-permute-start(bf16[768,512]{1,0:T(8,128)(2,1)S(1)} %get-tuple-element.15.refs_1_), channel_id=1, source_target_pairs={{0,2},{1,3},{2,0},{3,1},{4,6},{5,7},{6,4},{7,5},{8,10},{9,11},{10,... | collective-permute-start | bytes 2359304 | tf_op jit(solution)/shard_map/ppermute | solution.py:414
  32.3 5.9 %collective-permute-start.9 = (f32[2,32,128]{2,1,0:T(8,128)S(1)}, f32[2,32,128]{2,1,0:T(8,128)S(1)}, u32[]{:S(2)}, u32[]{:S(2)}) collective-permute-start(f32[2,32,128]{2,1,0:T(8,128)S(1)} %pad_maximum_fusion.refs_0_), channel_id=1, source_target_pairs={{0,24},{4,28},{8,16},{12,20},{16,8},{20,12},{24,0},{28,4},{1,25},{... | collective-permute-start | bytes 98312 | tf_op jit(solution)/shard_map/ppermute | solution.py:426
  35.9 4.8 %collective-permute-start.8 = (f32[2,32,128]{2,1,0:T(8,128)S(1)}, f32[2,32,128]{2,1,0:T(8,128)S(1)}, u32[]{:S(2)}, u32[]{:S(2)}) collective-permute-start(f32[2,32,128]{2,1,0:T(8,128)S(1)} %pad_maximum_fusion.refs_0_), channel_id=1, source_target_pairs={{0,16},{4,20},{8,24},{12,28},{16,0},{20,4},{24,8},{28,12},{1,17},{... | collective-permute-start | bytes 98312 | tf_op jit(solution)/shard_map/ppermute | solution.py:426
  35.9 4.8 %collective-permute-start.7 = (f32[2,32,128]{2,1,0:T(8,128)S(1)}, f32[2,32,128]{2,1,0:T(8,128)S(1)}, u32[]{:S(2)}, u32[]{:S(2)}) collective-permute-start(f32[2,32,128]{2,1,0:T(8,128)S(1)} %pad_maximum_fusion.refs_0_), channel_id=1, source_target_pairs={{0,8},{4,12},{8,0},{12,4},{16,24},{20,28},{24,16},{28,20},{1,9},{5... | collective-permute-start | bytes 98312 | tf_op jit(solution)/shard_map/ppermute | solution.py:426
  36.7 18.2 %collective-permute-start.4 = (bf16[256,512]{1,0:T(8,128)(2,1)S(1)}, bf16[256,512]{1,0:T(8,128)(2,1)S(1)}, u32[]{:S(2)}, u32[]{:S(2)}) collective-permute-start(bf16[256,512]{1,0:T(8,128)(2,1)S(1)} %get-tuple-element.11.refs_0_), channel_id=1, source_target_pairs={{0,2},{1,3},{2,0},{3,1},{4,6},{5,7},{6,4},{7,5},{8,10},{9,11},{10,... | collective-permute-start | bytes 786440 | tf_op jit(solution)/shard_map/ppermute | solution.py:410
  40.7 2.4 %copy-start.6 = (bf16[2,256,256]{2,1,0:T(8,128)(2,1)S(1)}, bf16[2,256,256]{2,1,0:T(8,128)(2,1)}, u32[]{:S(2)}) copy-start(bf16[2,256,256]{2,1,0:T(8,128)(2,1)} %constant.23.clone.row_t_ref) | copy-start | bytes 786436
  43.1 2.7 %collective-permute-start.10 = (f32[8,128]{1,0:T(8,128)S(1)}, f32[8,128]{1,0:T(8,128)S(1)}, u32[]{:S(2)}, u32[]{:S(2)}) collective-permute-start(f32[8,128]{1,0:T(8,128)S(1)} %get-tuple-element.17), channel_id=1, source_target_pairs={{0,1},{1,0},{2,3},{3,2},{4,5},{5,4},{6,7},{7,6},{8,9},{9,8},{10,11... | collective-permute-start | bytes 12296 | tf_op jit(solution)/shard_map/ppermute | solution.py:431
  45.9 7.7 %collective-permute-start.11 = (f32[8,128]{1,0:T(8,128)S(1)}, f32[8,128]{1,0:T(8,128)S(1)}, u32[]{:S(2)}, u32[]{:S(2)}) collective-permute-start(f32[8,128]{1,0:T(8,128)S(1)} %add.15), channel_id=1, source_target_pairs={{0,2},{1,3},{2,0},{3,1},{4,6},{5,7},{6,4},{7,5},{8,10},{9,11},{10,... | collective-permute-start | bytes 12296 | tf_op jit(solution)/shard_map/ppermute | solution.py:432
